TPU v7x, 512 devices: a whole 4x8x8 slice. The times are simulated.
512 devices in a mesh: dp: 8 (over y_hi, core), ep: 64 (over x, y_lo, z).
Axes of the slice: x: 4, y: 8 (y_hi: 4, y_lo: 2; y = y_hi * 2 + y_lo), z: 8, core: 2. Of those that a mesh axis runs over, the one named last changes fastest.
Arguments:
- hidden_in: bfloat16 [12288, 4096], P(('dp', 'ep')), may hold values from -6 to 6
- expert_ids: int32 [12288, 2], P(('dp', 'ep')), may hold values from 0 to 63, all different within a row; in each aligned block of 24 rows (0 to 23, 24 to 47, ...) at most 2 rows name the same one
- route_logits: float32 [12288, 64], P(('dp', 'ep')), may hold values from -10 to 10
- first_weight: bfloat16 [64, 4096, 1024], P('ep', None, 'dp'), may hold values from -0.09375 to 0.09375
- second_weight: bfloat16 [64, 1024, 4096], P('ep', None, 'dp'), may hold values from -0.1875 to 0.1875
- queries: bfloat16 [12288, 2048], P(('dp', 'ep')), may hold values from -140 to 140
- span_keys: bfloat16 [12288, 2048], P(('dp', 'ep')), may hold values from -7 to 7
- span_values: bfloat16 [12288, 2048], P(('dp', 'ep')), may hold values from -6 to 6
- cache_keys: bfloat16 [512, 72, 2048], P(('dp', 'ep')), may hold values from -6 to 6
- cache_values: bfloat16 [512, 72, 2048], P(('dp', 'ep')), may hold values from -6 to 6
- valid_frames: int32 [512], P(('dp', 'ep')), may hold values from 1 to 3
Outputs:
- mixed: bfloat16 [12288, 4096], P(('dp', 'ep'))
- attended: bfloat16 [12288, 2048], P(('dp', 'ep'))
Inputs may be any that keep to these rules, and one draw needn't show every extreme that they name: `expert_ids`: each token names two different experts. In the rows of one device (24 rows) no expert is named more than 2 times, a bound that some block reaches.
All inputs are finite; a program needn't handle non-finite values.
Results may differ from a plain program's by a relative error of at most 0.0057.
Values may be sent and summed in bfloat16 or wider, within the bound.
A program may use at most 128 MiB of HBM per device.

v0:
```python
import math
import jax
import jax.numpy as jnp
from jax import lax
from jax.sharding import PartitionSpec as P

HEADS = 16
HEAD_DIM = 128
FRAME_TOK = 24


def activate(pre):
    return jax.nn.gelu(pre, approximate=True).astype(jnp.bfloat16)


def expert_slots(expert_ids):
    flat_ids = expert_ids.reshape(-1)
    assigned = flat_ids.shape[0]
    row_ids = lax.broadcasted_iota(jnp.int32, (assigned, assigned), 0)
    col_ids = lax.broadcasted_iota(jnp.int32, (assigned, assigned), 1)
    same_expert = (flat_ids[:, None] == flat_ids[None, :]) & (col_ids < row_ids)
    return jnp.sum(same_expert.astype(jnp.int32), axis=1).reshape(expert_ids.shape)


def attend(queries, span_keys, span_values, cache_keys, cache_values, valid_count):
    token_count = queries.shape[0]
    cache_len = cache_keys.shape[0]
    key_rows = jnp.concatenate([cache_keys, span_keys], axis=0)
    value_rows = jnp.concatenate([cache_values, span_values], axis=0)
    query_heads = queries.reshape(token_count, HEADS, HEAD_DIM)
    key_heads = key_rows.reshape(-1, HEADS, HEAD_DIM)
    value_heads = value_rows.reshape(-1, HEADS, HEAD_DIM)
    scores = jnp.einsum(
        "thd,khd->htk", query_heads, key_heads, preferred_element_type=jnp.float32
    ) * (1.0 / math.sqrt(HEAD_DIM))
    position = lax.broadcasted_iota(jnp.int32, (key_rows.shape[0],), 0)
    usable = (position >= cache_len) | (position // FRAME_TOK < valid_count)
    scores = jnp.where(usable[None, None, :], scores, -1e30)
    row_max = jnp.max(scores, axis=2, keepdims=True)
    weights = jnp.exp(scores - row_max)
    weights = (weights / jnp.sum(weights, axis=2, keepdims=True)).astype(jnp.bfloat16)
    result = jnp.einsum("htk,khd->thd", weights, value_heads, preferred_element_type=jnp.float32)
    return result.astype(jnp.bfloat16).reshape(token_count, HEADS * HEAD_DIM)


def shards(
    hidden_in,
    expert_ids,
    route_logits,
    first_weight,
    second_weight,
    queries,
    span_keys,
    span_values,
    cache_keys,
    cache_values,
    valid_frames,
):
    tokens, model_width = hidden_in.shape
    experts = lax.axis_size("ep")
    capacity = max(2, 8 * tokens // (3 * experts))
    slots = expert_slots(expert_ids)
    places = expert_ids * capacity + slots
    place_ids = lax.broadcasted_iota(jnp.int32, (tokens, experts * capacity), 1)
    picks = [places[:, column : column + 1] == place_ids for column in range(2)]
    chooser = (picks[0] | picks[1]).astype(jnp.bfloat16)
    dispatch = lax.dot_general(
        chooser, hidden_in, (((0,), (0,)), ((), ())), preferred_element_type=jnp.float32
    )
    dispatch = dispatch.astype(jnp.bfloat16).reshape(experts, capacity, model_width)
    expert_cols = lax.broadcasted_iota(jnp.int32, route_logits.shape, 1)
    chosen = jnp.stack(
        [
            jnp.sum(
                jnp.where(expert_cols == expert_ids[:, column : column + 1], route_logits, 0.0),
                axis=1,
            )
            for column in range(2)
        ],
        axis=1,
    )
    gates = jax.nn.softmax(chosen, axis=1)
    first_local = first_weight[0]
    second_local = second_weight[0]
    received = lax.all_to_all(dispatch, "ep", split_axis=0, concat_axis=0, tiled=True)
    sources, item_count, _ = received.shape
    expert_rows = received.reshape(sources * item_count, model_width)
    hidden = activate(
        jnp.dot(
            expert_rows,
            lax.all_gather(first_local, "dp", axis=1, tiled=True),
            preferred_element_type=jnp.float32,
        )
    )
    result = jnp.dot(
        hidden,
        lax.all_gather(second_local, "dp", axis=1, tiled=True),
        preferred_element_type=jnp.float32,
    ).astype(jnp.bfloat16)
    outputs = result.reshape(sources, item_count, model_width)
    returned = lax.all_to_all(outputs, "ep", split_axis=0, concat_axis=0, tiled=True)
    attended = attend(
        queries, span_keys, span_values, cache_keys[0], cache_values[0], valid_frames[0]
    )
    flat_back = returned.reshape(experts * capacity, model_width)
    running = jnp.zeros((tokens, model_width), jnp.float32)
    for column in range(2):
        picked = jnp.dot(
            picks[column].astype(jnp.bfloat16), flat_back, preferred_element_type=jnp.float32
        )
        running = running + gates[:, column : column + 1] * picked
    mixed = running.astype(jnp.bfloat16)
    return (mixed, attended)


def solution(mesh):
    placed = (
        P(("dp", "ep"), None),
        P(("dp", "ep"), None),
        P(("dp", "ep"), None),
        P("ep", None, "dp"),
        P("ep", None, "dp"),
        P(("dp", "ep"), None),
        P(("dp", "ep"), None),
        P(("dp", "ep"), None),
        P(("dp", "ep"), None, None),
        P(("dp", "ep"), None, None),
        P(("dp", "ep")),
    )
    return jax.shard_map(
        shards,
        mesh=mesh,
        in_specs=placed,
        out_specs=(P(("dp", "ep"), None), P(("dp", "ep"), None)),
        check_vma=False,
    )
```

profile of v0, /device:TPU:2, one launch (start us, length us, event | category | flops | bytes accessed | tf_op | source)
XLA Modules:
  0.0 263.9 jit_solution(3099905430017032602)
XLA Ops:
  7.2 0.0 copy-start
  7.2 0.0 all-gather.7.cloned.1.call-start
  7.2 0.7 all-gather.7.cloned.1.call-update
  7.9 0.0 all-gather.5.cloned.1.call-start
  8.0 0.7 all-gather.5.cloned.1.call-update
  8.7 0.8 copy.35
  9.4 0.1 eq.61
  9.5 0.2 convert_reduce_fusion
  9.7 0.1 reshape.64
  9.8 0.1 copy.36
  9.9 0.7 multiply_add_fusion
  10.6 0.0 copy-done
  10.6 0.5 convolution_convert_fusion
  11.1 0.7 reshape.65
  11.9 52.7 %all_to_all.10 = bf16[64,2,4096]{2,1,0:T(2,128)(2,1)S(1)} all-to-all(bf16[64,2,4096]{2,1,0:T(2,128)(2,1)S(1)} %reshape.65), channel_id=1, replica_groups=mesh['dp'=8,'ep'=64] {'ep'}, dimensions={0} | all-to-all | bytes 2097152 | tf_op jit(solution)/shard_map/all_to_all | solution.py:85
  64.5 0.4 reshape.66
  64.9 0.0 copy-start.1
  65.0 0.0 copy-start.2
  65.0 0.0 copy-start.3
  65.0 0.0 copy-start.4
  65.0 0.0 copy-start.7
  65.0 45.3 %all-gather.7.cloned.1.call-done = bf16[1,1024,4096]{2,1,0:T(8,128)(2,1)} async-done(((bf16[1,1024,512]{2,1,0:T(8,128)(2,1)}), bf16[1,1024,4096]{2,1,0:T(8,128)(2,1)}) %all-gather.7.cloned.1.call-update) | async-done | bytes 8388624 | tf_op jit(solution)/shard_map/all_gather | solution.py:97
  110.3 95.3 %all-gather.5.cloned.1.call-done = bf16[1,4096,1024]{2,1,0:T(8,128)(2,1)} async-done(((bf16[1,4096,128]{2,1,0:T(8,128)(2,1)}), bf16[1,4096,1024]{2,1,0:T(8,128)(2,1)}) %all-gather.5.cloned.1.call-update) | async-done | bytes 8388624 | tf_op jit(solution)/shard_map/all_gather | solution.py:91
  205.7 8.3 %fusion.5 = bf16[128,4096]{1,0:T(8,128)(2,1)S(1)} fusion(bf16[1,1024,4096]{2,1,0:T(8,128)(2,1)} %all-gather.7.cloned.1.call-done, bf16[128,4096]{1,0:T(8,128)(2,1)S(1)} %reshape.66, bf16[1,4096,1024]{2,1,0:T(8,128)(2,1)} %all-gather.5.cloned.1.call-done), kind=kOutput, calls=%fused_computation.5 | convolution fusion | flops 2149187584 | bytes 18874368 | tf_op jit(solution)/shard_map/dot_general | solution.py:95
  214.0 0.0 copy-start.6
  214.0 0.0 copy-start.5
  214.0 1.5 reshape.67
  215.5 10.9 %all-to-all-start.1 = ((bf16[64,2,4096]{2,1,0:T(2,128)(2,1)}), bf16[64,2,4096]{2,1,0:T(2,128)(2,1)S(1)}, u32[]{:S(2)}, u32[]{:S(2)}) async-start(bf16[64,2,4096]{2,1,0:T(2,128)(2,1)} %reshape.67), calls=%async_computation.1 | async-start | bytes 2097152 | tf_op jit(solution)/shard_map/all_to_all | solution.py:101
  226.4 0.0 copy-done.1
  226.5 0.1 copy.37
  226.6 0.0 copy-done.2
  226.6 0.1 copy.39
  227.4 0.0 copy-done.3
  227.4 0.0 copy-done.4
  227.5 0.0 copy-done.7
  227.5 0.5 fusion.70
  227.9 0.3 fusion.14
  228.2 0.7 copy.62
  228.9 0.0 copy-done.6
  228.9 0.0 copy-done.5
  228.9 0.2 select_reduce_fusion
  229.2 26.1 %all-to-all-done.1 = bf16[64,2,4096]{2,1,0:T(2,128)(2,1)S(1)} async-done(((bf16[64,2,4096]{2,1,0:T(2,128)(2,1)}), bf16[64,2,4096]{2,1,0:T(2,128)(2,1)S(1)}, u32[]{:S(2)}, u32[]{:S(2)}) %all-to-all-start.1) | async-done | bytes 1048608 | tf_op jit(solution)/shard_map/all_to_all | solution.py:101
  255.3 0.4 reshape.68
  255.7 0.3 convolution_multiply_fusion.1
  256.0 1.0 fusion.9
  (11 shorter events, 0.2 us)
Async XLA Ops:
  7.2 3.4 %copy-start = (bf16[24,4096]{1,0:T(8,128)(2,1)S(1)}, bf16[24,4096]{1,0:T(8,128)(2,1)}, u32[]{:S(2)}) copy-start(bf16[24,4096]{1,0:T(8,128)(2,1)} %param.11) | copy-start | bytes 589828
  7.2 103.1 %all-gather.7.cloned.1.call-start = ((), (), s32[]{:S(2)}) async-start(), calls=%async_computation.3 | async-start | bytes 9437184 | tf_op jit(solution)/shard_map/all_gather | solution.py:97
  7.9 197.7 %all-gather.5.cloned.1.call-start = ((), (), s32[]{:S(2)}) async-start(), calls=%async_computation.2 | async-start | bytes 9437184 | tf_op jit(solution)/shard_map/all_gather | solution.py:91
  64.9 161.5 %copy-start.1 = (bf16[1,72,2048]{2,1,0:T(8,128)(2,1)S(1)}, bf16[1,72,2048]{2,1,0:T(8,128)(2,1)}, u32[]{:S(2)}) copy-start(bf16[1,72,2048]{2,1,0:T(8,128)(2,1)} %param.20) | copy-start | bytes 884740
  65.0 161.6 %copy-start.2 = (bf16[1,72,2048]{2,1,0:T(8,128)(2,1)S(1)}, bf16[1,72,2048]{2,1,0:T(8,128)(2,1)}, u32[]{:S(2)}) copy-start(bf16[1,72,2048]{2,1,0:T(8,128)(2,1)} %param.19) | copy-start | bytes 884740
  65.0 162.4 %copy-start.3 = (bf16[24,2048]{1,0:T(8,128)(2,1)S(1)}, bf16[24,2048]{1,0:T(8,128)(2,1)}, u32[]{:S(2)}) copy-start(bf16[24,2048]{1,0:T(8,128)(2,1)} %param.18) | copy-start | bytes 294916
  65.0 162.4 %copy-start.4 = (bf16[24,2048]{1,0:T(8,128)(2,1)S(1)}, bf16[24,2048]{1,0:T(8,128)(2,1)}, u32[]{:S(2)}) copy-start(bf16[24,2048]{1,0:T(8,128)(2,1)} %param.17) | copy-start | bytes 294916
  65.0 162.5 %copy-start.7 = (bf16[24,2048]{1,0:T(8,128)(2,1)S(1)}, bf16[24,2048]{1,0:T(8,128)(2,1)}, u32[]{:S(2)}) copy-start(bf16[24,2048]{1,0:T(8,128)(2,1)} %param.16) | copy-start | bytes 294916
  214.0 14.9 %copy-start.6 = (s32[24,2]{0,1:T(2,128)S(1)}, s32[24,2]{0,1:T(2,128)}, u32[]{:S(2)}) copy-start(s32[24,2]{0,1:T(2,128)} %param.12) | copy-start | bytes 580
  214.0 14.9 %copy-start.5 = (f32[24,64]{1,0:T(8,128)S(1)}, f32[24,64]{1,0:T(8,128)}, u32[]{:S(2)}) copy-start(f32[24,64]{1,0:T(8,128)} %param.13) | copy-start | bytes 18436
  215.5 39.8 %all-to-all-start.1 = ((bf16[64,2,4096]{2,1,0:T(2,128)(2,1)}), bf16[64,2,4096]{2,1,0:T(2,128)(2,1)S(1)}, u32[]{:S(2)}, u32[]{:S(2)}) async-start(bf16[64,2,4096]{2,1,0:T(2,128)(2,1)} %reshape.67), calls=%async_computation.1 | async-start | bytes 2097152 | tf_op jit(solution)/shard_map/all_to_all | solution.py:101
Sparse Core Ops, SparseCore 0:
  10.1 100.1 all-gather.6
  112.4 93.1 all-gather.4
where the time goes:
time: 264 us
  waiting for transfers between devices  168 us (64%)
  blocking collectives  52.7 us (20%)
  between operations  14.9 us (6%)
  starting transfers between devices  11 us (4%)
  matrix products  10.9 us (4%)
  local copies, waits for them, and re-layouts  5.07 us (2%)
    all_gather x1, waiting for transfers between devices, shards(): lax.all_gather(first_local, 'dp', axis=1, tiled=True)  95.3 us
    all_to_all x1, blocking collectives, shards(): lax.all_to_all(dispatch, 'ep', split_axis=0, concat_axis=0, tiled=True)  52.7 us
    all_gather x1, waiting for transfers between devices, shards(): lax.all_gather(second_local, 'dp', axis=1, tiled=True)  45.3 us
    all_to_all x1, waiting for transfers between devices, shards(): lax.all_to_all(outputs, 'ep', split_axis=0, concat_axis=0, tiled=True)  26.1 us
    all_to_all x1, starting transfers between devices, shards(): lax.all_to_all(outputs, 'ep', split_axis=0, concat_axis=0, tiled=True)  10.9 us
    dot_general x1, matrix products, shards(): jnp.dot(hidden, lax.all_gather(second_local, 'dp', axis=1, tiled=True), p...  8.33 us
  transfers between devices with their start and end apart: 3, of which 3 were waited for; matrix products, arithmetic and copies ran while one was open for 2% of the time, Pallas kernels for 0%

commit v1 on v0

--- a/solution.py
+++ b/solution.py
@@ -88,7 +88,9 @@
     hidden = activate(
         jnp.dot(
             expert_rows,
-            lax.all_gather(first_local, "dp", axis=1, tiled=True),
+            jnp.concatenate(
+                lax.all_to_all(jnp.stack([first_local] * lax.axis_size("dp")), "dp", 0, 0), axis=1
+            ),
             preferred_element_type=jnp.float32,
         )
     )

time: 264 us -> 374 us (1.42)
  waiting for transfers between devices: 168 us -> 306 us
  blocking collectives: 52.7 us -> 0 us
  starting transfers between devices: 11 us -> 26.7 us
  local copies, waits for them, and re-layouts: 5.07 us -> 11.8 us
    all_to_all x0 -> x2, waiting for transfers between devices: none -> 280 us  [the longest x1 253 us: shards(): lax.all_to_all(jnp.stack([first_local] * lax.axis_size('dp')), 'dp', 0, 0)]
    all_gather x1 -> x0, waiting for transfers between devices: 95.3 us -> none  [shards(): lax.all_gather(first_local, 'dp', axis=1, tiled=True)]
    all_to_all x1 -> x0, blocking collectives: 52.7 us -> none  [shards(): lax.all_to_all(dispatch, 'ep', split_axis=0, concat_axis=0, tiled=True)]
    all_gather x1, waiting for transfers between devices: 45.3 us -> 0.01 us  [shards(): lax.all_gather(second_local, 'dp', axis=1, tiled=True)]
    all_to_all x0 -> x2, starting transfers between devices: none -> 21.1 us  [the longest x1 14.9 us: shards(): lax.all_to_all(dispatch, 'ep', split_axis=0, concat_axis=0, tiled=True)]
    another operation x0 -> x2, local copies, waits for them, and re-layouts: none -> 5.83 us  [the longest x1 4.35 us: shards(): jnp.stack([first_local] * lax.axis_size('dp'))]
    all_to_all x1, starting transfers between devices: 10.9 us -> 5.55 us  [shards(): lax.all_to_all(outputs, 'ep', split_axis=0, concat_axis=0, tiled=True)]
  transfers between devices with their start and end apart: 3 -> 4, of which waited for: 3 -> 3; matrix products, arithmetic and copies ran while one was open for 2% -> 1% of each run, Pallas kernels for 0% -> 0%
where the time goes in v1:
time: 374 us; the launch traced here: 373 us
  waiting for transfers between devices  306 us (82%)
  starting transfers between devices  26.7 us (7%)
  between operations  14.9 us (4%)
  matrix products  12.6 us (3%)
  local copies, waits for them, and re-layouts  11.8 us (3%)
    all_to_all x1, waiting for transfers between devices, shards(): lax.all_to_all(jnp.stack([first_local] * lax.axis_size('dp')), 'dp', 0, 0)  253 us
    all_to_all x1, waiting for transfers between devices, shards(): lax.all_to_all(dispatch, 'ep', split_axis=0, concat_axis=0, tiled=True)  27 us
    all_to_all x1, waiting for transfers between devices, shards(): lax.all_to_all(outputs, 'ep', split_axis=0, concat_axis=0, tiled=True)  25.4 us
    all_to_all x1, starting transfers between devices, shards(): lax.all_to_all(dispatch, 'ep', split_axis=0, concat_axis=0, tiled=True)  14.9 us
    dot_general x1, matrix products, shards(): jnp.dot(hidden, lax.all_gather(second_local, 'dp', axis=1, tiled=True), p...  9.95 us
  transfers between devices with their start and end apart: 4, of which 3 were waited for; matrix products, arithmetic and copies ran while one was open for 1% of the time, Pallas kernels for 0%

profile of v1, /device:TPU:2, one launch (start us, length us, event | category | flops | bytes accessed | tf_op | source)
XLA Modules:
  0.0 373.2 jit_solution(10964587880860550526)
XLA Ops:
  7.2 0.0 copy-start
  7.2 0.8 copy.37
  8.0 0.1 eq.61
  8.1 0.2 convert_reduce_fusion
  8.3 0.1 reshape.71
  8.4 0.1 copy.38
  8.4 0.7 multiply_add_fusion
  9.1 0.0 copy-done
  9.1 0.5 convolution_convert_fusion
  9.7 1.5 reshape.72
  11.2 14.9 %all-to-all-start = ((bf16[64,2,4096]{2,1,0:T(2,128)(2,1)}), bf16[64,2,4096]{2,1,0:T(2,128)(2,1)S(1)}, u32[]{:S(2)}, u32[]{:S(2)}) async-start(bf16[64,2,4096]{2,1,0:T(2,128)(2,1)} %reshape.72), calls=%async_computation | async-start | bytes 2097152 | tf_op jit(solution)/shard_map/all_to_all | solution.py:85
  26.1 1.5 copy.39
  27.6 27.0 %all-to-all-done = bf16[64,2,4096]{2,1,0:T(2,128)(2,1)S(1)} async-done(((bf16[64,2,4096]{2,1,0:T(2,128)(2,1)}), bf16[64,2,4096]{2,1,0:T(2,128)(2,1)S(1)}, u32[]{:S(2)}, u32[]{:S(2)}) %all-to-all-start) | async-done | bytes 1048608 | tf_op jit(solution)/shard_map/all_to_all | solution.py:85
  54.6 4.3 %stack.15 = bf16[8,4096,128]{1,2,0:T(8,128)(2,1)} broadcast(bf16[4096,128]{0,1:T(8,128)(2,1)S(1)} %copy.39), dimensions={1,2} | broadcast | bytes 9437184 | tf_op jit(solution)/shard_map/stack | solution.py:92
  58.9 6.2 %all-to-all-start.1 = ((bf16[8,4096,128]{1,2,0:T(8,128)(2,1)}), bf16[8,4096,128]{1,2,0:T(8,128)(2,1)}, u32[]{:S(2)}, u32[]{:S(2)}) async-start(bf16[8,4096,128]{1,2,0:T(8,128)(2,1)} %stack.15), calls=%async_computation.1 | async-start | bytes 16777216 | tf_op jit(solution)/shard_map/all_to_all | solution.py:92
  65.1 0.0 all-gather.3.cloned.1.call-start
  65.2 0.7 all-gather.3.cloned.1.call-update
  65.8 0.4 reshape.73
  66.3 253.1 %all-to-all-done.1 = bf16[8,4096,128]{1,2,0:T(8,128)(2,1)} async-done(((bf16[8,4096,128]{1,2,0:T(8,128)(2,1)}), bf16[8,4096,128]{1,2,0:T(8,128)(2,1)}, u32[]{:S(2)}, u32[]{:S(2)}) %all-to-all-start.1) | async-done | bytes 8388640 | tf_op jit(solution)/shard_map/all_to_all | solution.py:92
  319.4 0.0 all-gather.3.cloned.1.call-done
  319.4 0.0 copy-start.1
  319.4 0.0 copy-start.2
  319.4 0.0 copy-start.3
  319.4 0.0 copy-start.4
  319.4 0.0 copy-start.7
  319.4 9.9 %fusion.3 = bf16[128,4096]{1,0:T(8,128)(2,1)S(1)} fusion(bf16[1,1024,4096]{2,1,0:T(8,128)(2,1)} %all-gather.3.cloned.1.call-done, bf16[128,4096]{1,0:T(8,128)(2,1)S(1)} %reshape.73, bf16[4096,1024]{0,1:T(8,128)(2,1)} %bitcast.9), kind=kOutput, calls=%fused_computation.3 | convolution fusion | flops 2149187584 | bytes 18874368 | tf_op jit(solution)/shard_map/dot_general | solution.py:97
  329.4 0.0 copy-start.6
  329.4 0.0 copy-start.5
  329.4 1.5 reshape.76
  330.9 5.6 %all-to-all-start.2 = ((bf16[64,2,4096]{2,1,0:T(2,128)(2,1)}), bf16[64,2,4096]{2,1,0:T(2,128)(2,1)S(1)}, u32[]{:S(2)}, u32[]{:S(2)}) async-start(bf16[64,2,4096]{2,1,0:T(2,128)(2,1)} %reshape.76), calls=%async_computation.2 | async-start | bytes 2097152 | tf_op jit(solution)/shard_map/all_to_all | solution.py:103
  336.5 0.0 copy-done.1
  336.5 0.1 copy.42
  337.3 0.0 copy-done.2
  337.3 0.1 copy.40
  337.4 0.0 copy-done.3
  337.5 0.0 copy-done.4
  337.5 0.0 copy-done.7
  337.5 0.5 fusion.63
  338.0 0.3 fusion.12
  338.3 0.7 copy.65
  338.9 0.0 copy-done.6
  339.0 0.0 copy-done.5
  339.0 0.2 select_reduce_fusion
  339.2 25.4 %all-to-all-done.2 = bf16[64,2,4096]{2,1,0:T(2,128)(2,1)S(1)} async-done(((bf16[64,2,4096]{2,1,0:T(2,128)(2,1)}), bf16[64,2,4096]{2,1,0:T(2,128)(2,1)S(1)}, u32[]{:S(2)}, u32[]{:S(2)}) %all-to-all-start.2) | async-done | bytes 1048608 | tf_op jit(solution)/shard_map/all_to_all | solution.py:103
  364.6 0.4 reshape.77
  365.0 0.3 convolution_multiply_fusion.1
  365.3 1.0 fusion.7
  (11 shorter events, 0.2 us)
Async XLA Ops:
  7.2 2.0 copy-start
  11.2 43.4 %all-to-all-start = ((bf16[64,2,4096]{2,1,0:T(2,128)(2,1)}), bf16[64,2,4096]{2,1,0:T(2,128)(2,1)S(1)}, u32[]{:S(2)}, u32[]{:S(2)}) async-start(bf16[64,2,4096]{2,1,0:T(2,128)(2,1)} %reshape.72), calls=%async_computation | async-start | bytes 2097152 | tf_op jit(solution)/shard_map/all_to_all | solution.py:85
  58.9 260.5 %all-to-all-start.1 = ((bf16[8,4096,128]{1,2,0:T(8,128)(2,1)}), bf16[8,4096,128]{1,2,0:T(8,128)(2,1)}, u32[]{:S(2)}, u32[]{:S(2)}) async-start(bf16[8,4096,128]{1,2,0:T(8,128)(2,1)} %stack.15), calls=%async_computation.1 | async-start | bytes 16777216 | tf_op jit(solution)/shard_map/all_to_all | solution.py:92
  65.1 254.3 %all-gather.3.cloned.1.call-start = ((), (), s32[]{:S(2)}) async-start(), calls=%async_computation.3 | async-start | bytes 9437184 | tf_op jit(solution)/shard_map/all_gather | solution.py:99
  319.4 17.1 %copy-start.1 = (bf16[1,72,2048]{2,1,0:T(8,128)(2,1)S(1)}, bf16[1,72,2048]{2,1,0:T(8,128)(2,1)}, u32[]{:S(2)}) copy-start(bf16[1,72,2048]{2,1,0:T(8,128)(2,1)} %param.19) | copy-start | bytes 884740
  319.4 17.9 %copy-start.2 = (bf16[1,72,2048]{2,1,0:T(8,128)(2,1)S(1)}, bf16[1,72,2048]{2,1,0:T(8,128)(2,1)}, u32[]{:S(2)}) copy-start(bf16[1,72,2048]{2,1,0:T(8,128)(2,1)} %param.20) | copy-start | bytes 884740
  319.4 18.0 %copy-start.3 = (bf16[24,2048]{1,0:T(8,128)(2,1)S(1)}, bf16[24,2048]{1,0:T(8,128)(2,1)}, u32[]{:S(2)}) copy-start(bf16[24,2048]{1,0:T(8,128)(2,1)} %param.17) | copy-start | bytes 294916
  319.4 18.1 %copy-start.4 = (bf16[24,2048]{1,0:T(8,128)(2,1)S(1)}, bf16[24,2048]{1,0:T(8,128)(2,1)}, u32[]{:S(2)}) copy-start(bf16[24,2048]{1,0:T(8,128)(2,1)} %param.18) | copy-start | bytes 294916
  319.4 18.1 %copy-start.7 = (bf16[24,2048]{1,0:T(8,128)(2,1)S(1)}, bf16[24,2048]{1,0:T(8,128)(2,1)}, u32[]{:S(2)}) copy-start(bf16[24,2048]{1,0:T(8,128)(2,1)} %param.16) | copy-start | bytes 294916
  329.4 9.6 %copy-start.6 = (s32[24,2]{0,1:T(2,128)S(1)}, s32[24,2]{0,1:T(2,128)}, u32[]{:S(2)}) copy-start(s32[24,2]{0,1:T(2,128)} %param.12) | copy-start | bytes 580
  329.4 9.6 %copy-start.5 = (f32[24,64]{1,0:T(8,128)S(1)}, f32[24,64]{1,0:T(8,128)}, u32[]{:S(2)}) copy-start(f32[24,64]{1,0:T(8,128)} %param.13) | copy-start | bytes 18436
  330.9 33.7 %all-to-all-start.2 = ((bf16[64,2,4096]{2,1,0:T(2,128)(2,1)}), bf16[64,2,4096]{2,1,0:T(2,128)(2,1)S(1)}, u32[]{:S(2)}, u32[]{:S(2)}) async-start(bf16[64,2,4096]{2,1,0:T(2,128)(2,1)} %reshape.76), calls=%async_computation.2 | async-start | bytes 2097152 | tf_op jit(solution)/shard_map/all_to_all | solution.py:103
Sparse Core Ops, SparseCore 0:
  68.0 189.5 all-gather.2
